TPU v7x, 32 devices: a whole 2x2x4 slice. The times are simulated.
32 devices in a mesh: dp: 4 (over x, core), vocab: 8 (over z, y).
Axes of the slice: x: 2, y: 2, z: 4, core: 2. Of those that a mesh axis runs over, the one named last changes fastest.
Arguments:
- hidden: bfloat16 [256, 4608], P(('dp', 'vocab')), may hold values from -6 to 6
- embedding: bfloat16 [4096, 4608], P('vocab'), may hold values from -0.25 to 0.25
- targets: int32 [256], P('dp'), may hold values from 0 to 4095
- grammar_bits: int32 [256, 128], P('dp', 'vocab'), may hold values from -2147483648 to 2147483647, as said below
Outputs:
- token_loss: float32 [256], P('dp')
- hidden_grad: float32 [256, 4608], P(('dp', 'vocab'))
- embed_grad: float32 [4096, 4608], P('vocab', 'dp')
Inputs may be any that keep to these rules, and one draw needn't show every extreme that they name: `grammar_bits`: bit b of word k of a token's row stands for vocabulary entry 32 k + b. Each 128-entry block of a row is either drawn at random or all zero, with a share of zero blocks that differs from block to block of the vocabulary.
All inputs are finite; a program needn't handle non-finite values.
Results may differ from a plain program's by a relative error of at most 0.0023.
Values may be sent and summed in bfloat16 or wider, within the bound.
A program may use at most 128 MiB of HBM per device.

v0:
```python
import jax
import jax.numpy as jnp
from jax import lax
from jax.sharding import PartitionSpec as P

softcap = 30.0


def score_rows(rows_piece, embedding):
    return lax.dot_general(
        rows_piece, embedding, (((1,), (1,)), ((), ())), preferred_element_type=jnp.float32
    )


def on_device(hidden, embedding, targets, grammar_bits):
    vocab_local = embedding.shape[0]
    vocab_start = lax.axis_index("vocab") * vocab_local
    gathered = lax.all_gather(hidden, "vocab", axis=0, tiled=True)
    scores = score_rows(gathered, embedding)
    row_count = scores.shape[0]
    capped = softcap * jnp.tanh(scores / softcap)
    shifts = jnp.arange(32, dtype=jnp.int32)
    unpacked = jnp.right_shift(grammar_bits[:, :, None], shifts[None, None, :]) & 1
    unpacked = unpacked.reshape(row_count, vocab_local)
    vocab_ids = vocab_start + jnp.arange(vocab_local, dtype=jnp.int32)
    onehot = vocab_ids[None, :] == targets[:, None]
    allowed = (unpacked == 1) | onehot
    local_total = jnp.sum(jnp.where(allowed, jnp.exp(capped), 0.0), axis=1)
    local_target = jnp.sum(jnp.where(onehot, capped, 0.0), axis=1)
    totals, target_logit = lax.psum((local_total, local_target), "vocab")
    log_total = jnp.log(totals)
    token_loss = log_total - target_logit
    probability = jnp.where(allowed, jnp.exp(capped - log_total[:, None]), 0.0)
    softcap_slope = 1.0 - jnp.square(capped / softcap)
    dlogit = ((probability - onehot.astype(jnp.float32)) * softcap_slope).astype(jnp.bfloat16)
    hidden_grad = lax.psum_scatter(
        jnp.dot(dlogit, embedding, preferred_element_type=jnp.float32),
        "vocab",
        scatter_dimension=0,
        tiled=True,
    )
    data_count = lax.axis_size("dp")
    group_count = lax.axis_size("vocab")
    tok_local = hidden.shape[0]
    column_block = lax.all_to_all(hidden, "dp", split_axis=1, concat_axis=0, tiled=True)
    all_dlogit = lax.all_gather(dlogit, "dp", axis=0, tiled=True)
    ordered = all_dlogit.reshape(data_count, group_count, tok_local, vocab_local)
    ordered = jnp.transpose(ordered, (1, 0, 2, 3)).reshape(
        data_count * group_count * tok_local, vocab_local
    )
    embed_grad = lax.dot_general(
        ordered,
        lax.all_gather(column_block, "vocab", axis=0, tiled=True),
        (((0,), (0,)), ((), ())),
        preferred_element_type=jnp.float32,
    )
    return (token_loss, hidden_grad, embed_grad)


def solution(mesh):
    in_specs = (P(("dp", "vocab"), None), P("vocab", None), P("dp"), P("dp", "vocab"))
    out_specs = (P("dp"), P(("dp", "vocab"), None), P("vocab", "dp"))
    return jax.shard_map(
        on_device, mesh=mesh, in_specs=in_specs, out_specs=out_specs, check_vma=False
    )
```

profile of v0, /device:TPU:0, one launch (start us, length us, event | category | flops | bytes accessed | tf_op | source)
XLA Modules:
  0.0 143.0 jit_solution(13688086459809105506)
XLA Ops:
  7.2 0.0 copy-start
  7.2 0.0 reduce-scatter.2.cloned.1.call-start
  7.2 0.1 shift_right_arithmetic.23
  7.3 0.7 shift_right_arithmetic.20
  8.0 0.1 copy.8
  8.2 33.5 %all_gather.9 = bf16[64,4608]{1,0:T(8,128)(2,1)S(1)} all-gather(bf16[8,4608]{1,0:T(8,128)(2,1)} %param.4), channel_id=1, replica_groups=mesh['dp'=4,'vocab'=8] {'vocab'}, dimensions={0}, use_global_device_ids=true | all-gather | bytes 663552 | tf_op jit(solution)/shard_map/all_gather | solution.py:18
  41.6 4.0 %select_reduce_fusion = (f32[64]{0:T(128)S(1)}, f32[64]{0:T(128)S(1)}, pred[64,512]{1,0:T(8,128)(4,1)S(1)}, f32[64,512]{1,0:T(8,128)S(1)}) fusion(s32[64]{0:T(128)} %param.6, s32[512]{0:T(512)S(1)} %iota_add_fusion, s32[64,512]{1,0:T(8,128)S(1)} %copy.8, s32[512]{0:T(512)S(1)} %shift_right_arithmetic.23, bf16[64,4608]{1,0:T(8,128)(2,1)S(1)} %all_gather.9, ...), kind=kOutput, calls=%fused_computation.9 | convolution fusion | flops 302350208 | bytes 5608192 | tf_op jit(solution)/shard_map/dot_general | solution.py:10
  45.7 21.5 %all-reduce = (f32[64]{0:T(128)S(1)}, f32[64]{0:T(128)S(1)}) all-reduce(f32[64]{0:T(128)S(1)} %get-tuple-element.4, f32[64]{0:T(128)S(1)} %get-tuple-element.3), channel_id=1, replica_groups=mesh['dp'=4,'vocab'=8] {'vocab'}, use_global_device_ids=true, to_apply=%region_3.4 | all-reduce | flops 128 | bytes 1024 | tf_op jit(solution)/shard_map/psum | solution.py:30
  67.1 0.5 fusion.5
  67.6 0.0 copy-done
  67.6 0.1 fusion.4
  67.8 4.3 %fusion.6 = f32[64,4608]{1,0:T(8,128)} fusion(bf16[64,512]{1,0:T(8,128)(2,1)S(1)} %fusion.4, bf16[512,4608]{1,0:T(8,128)(2,1)} %param.5), kind=kOutput, calls=%fused_computation.14 | convolution fusion | flops 301989888 | bytes 5963776 | tf_op jit(solution)/shard_map/dot_general | solution.py:37
  72.0 0.0 reduce-scatter.2.cloned.1.call-update
  72.1 3.3 %all-to-all-start = ((bf16[8,4,1152]{2,0,1:T(8,128)(2,1)}), bf16[8,4,1152]{2,0,1:T(8,128)(2,1)S(1)}, u32[]{:S(2)}, u32[]{:S(2)}) async-start(bf16[8,4,1152]{2,0,1:T(8,128)(2,1)} %bitcast.4), calls=%async_computation.1 | async-start | bytes 147456 | tf_op jit(solution)/shard_map/all_to_all | solution.py:45
  75.4 6.4 %all_gather.10 = bf16[256,512]{1,0:T(8,128)(2,1)S(1)} all-gather(bf16[64,512]{1,0:T(8,128)(2,1)S(1)} %fusion.4), channel_id=1, replica_groups=mesh['dp'=4,'vocab'=8] {'dp'}, dimensions={0}, use_global_device_ids=true | all-gather | bytes 327680 | tf_op jit(solution)/shard_map/all_gather | solution.py:46
  81.8 0.0 all-to-all-done
  81.8 32.1 %all_gather.11 = bf16[256,1152]{1,0:T(8,128)(2,1)S(1)} all-gather(bf16[32,1152]{1,0:T(8,128)(2,1)S(1)} %bitcast.18), channel_id=1, replica_groups=mesh['dp'=4,'vocab'=8] {'vocab'}, dimensions={0}, use_global_device_ids=true | all-gather | bytes 663552 | tf_op jit(solution)/shard_map/all_gather | solution.py:53
  113.9 1.9 %fusion.7 = f32[512,1152]{1,0:T(8,128)} fusion(bf16[256,512]{1,0:T(8,128)(2,1)S(1)} %bitcast.15, bf16[256,1152]{1,0:T(8,128)(2,1)S(1)} %all_gather.11), kind=kOutput, calls=%fused_computation.15 | convolution fusion | flops 301989888 | bytes 3211264 | tf_op jit(solution)/shard_map/dot_general | solution.py:51
  115.9 20.3 %reduce-scatter.2.cloned.1.call-done = f32[8,4608]{1,0:T(8,128)} async-done(((f32[64,4608]{1,0:T(8,128)}), f32[8,4608]{1,0:T(8,128)}) %reduce-scatter.2.cloned.1.call-update) | async-done | bytes 147472 | tf_op jit(solution)/shard_map/reduce_scatter | solution.py:36
  (3 shorter events, 0.0 us)
Async XLA Ops:
  7.2 60.5 %copy-start = (s32[64]{0:T(128)S(1)}, s32[64]{0:T(128)}, u32[]{:S(2)}) copy-start(s32[64]{0:T(128)} %param.6) | copy-start | bytes 772
  7.2 128.9 %reduce-scatter.2.cloned.1.call-start = ((), (), s32[]{:S(2)}) async-start(), calls=%async_computation.2 | async-start | bytes 1327104 | tf_op jit(solution)/shard_map/reduce_scatter | solution.py:36
  72.1 9.7 %all-to-all-start = ((bf16[8,4,1152]{2,0,1:T(8,128)(2,1)}), bf16[8,4,1152]{2,0,1:T(8,128)(2,1)S(1)}, u32[]{:S(2)}, u32[]{:S(2)}) async-start(bf16[8,4,1152]{2,0,1:T(8,128)(2,1)} %bitcast.4), calls=%async_computation.1 | async-start | bytes 147456 | tf_op jit(solution)/shard_map/all_to_all | solution.py:45
Sparse Core Ops, SparseCore 0:
  72.2 63.8 reduce-scatter.1
where the time goes:
time: 143 us
  blocking collectives  93.4 us (65%)
  waiting for transfers between devices  20.3 us (14%)
  between operations  14.1 us (10%)
  matrix products  10.2 us (7%)
  starting transfers between devices  3.34 us (2%)
    all_gather x1, blocking collectives, on_device(): gathered = lax.all_gather(hidden, 'vocab', axis=0, tiled=True)  33.5 us
    all_gather x1, blocking collectives, on_device(): lax.all_gather(column_block, 'vocab', axis=0, tiled=True)  32.1 us
    psum x1, blocking collectives, on_device(): totals, target_logit = lax.psum((local_total, local_target), 'vocab')  21.5 us
    reduce_scatter x1, waiting for transfers between devices, on_device(): lax.psum_scatter(jnp.dot(dlogit, embedding, preferred_element_type=jnp.fl...  20.3 us
    all_gather x1, blocking collectives, on_device(): all_dlogit = lax.all_gather(dlogit, 'dp', axis=0, tiled=True)  6.37 us
    dot_general x1, matrix products, on_device(): jnp.dot(dlogit, embedding, preferred_element_type=jnp.float32)  4.28 us
    dot_general x1, matrix products, score_rows(): lax.dot_general(rows_piece, embedding, (((1,), (1,)), ((), ())), preferre...  4.02 us
    all_to_all x1, starting transfers between devices, on_device(): lax.all_to_all(hidden, 'dp', split_axis=1, concat_axis=0, tiled=True)  3.3 us
  transfers between devices with their start and end apart: 2, of which 1 were waited for; matrix products, arithmetic and copies ran while one was open for 1% of the time, Pallas kernels for 0%

commit v1 on v0

v1 whole, which is shorter than its diff:
```python
import functools

import jax
import jax.numpy as jnp
from jax import lax
from jax.experimental import pallas as pl
from jax.experimental.pallas import tpu as pltpu
from jax.sharding import PartitionSpec as P

softcap = 30.0
MESH = pl.DeviceIdType.MESH
f32 = jnp.float32
bf16 = jnp.bfloat16


def kernel(
    data, outer, inner,
    hidden_hbm, embed_hbm, targets_hbm, bits_hbm,
    loss_ref, hgrad_ref, egrad_hbm,
    own, emb, tgt, bits, gath, cols, dl, h2, stat, stat_in,
    part, y_out, y_in, total, z_out, z_in, egrad, allow, hot,
    local_sem, emb_sem, place_sem, egrad_sem,
    gz_s, gz_r, gy_s, gy_r, gd_s, gd_r, st_s, st_r, dl_s, dl_r,
    ry_s, ry_r, rz_s, rz_r,
):
    d = lax.axis_index("dp")
    v = lax.axis_index("vocab")
    group = outer * inner
    a, b = v // inner, v % inner
    rows, width = own.shape[0], emb.shape[2]
    vocab_local = emb.shape[1]
    tokens = group * rows

    def at_outer(i):
        return ((a + i) % outer) * inner + b

    def at_inner(i):
        return a * inner + (b + i) % inner

    def columns(j):
        return pl.ds(pl.multiple_of(j * width, 128), width)

    def remote(src, dst, send, recv, **where):
        return pltpu.make_async_remote_copy(
            src_ref=src, dst_ref=dst, send_sem=send, recv_sem=recv,
            device_id=where, device_id_type=MESH,
        )

    order = [(d + 1 + k) % data for k in range(data)]
    own_copy = pltpu.make_async_copy(hidden_hbm, own, local_sem.at[0])
    own_copy.start()
    tgt_copy = pltpu.make_async_copy(targets_hbm, tgt, local_sem.at[1])
    tgt_copy.start()
    bits_copy = pltpu.make_async_copy(bits_hbm, bits, local_sem.at[2])
    bits_copy.start()
    barrier = pltpu.get_barrier_semaphore()
    for i in range(1, group):
        pl.semaphore_signal(barrier, inc=1, device_id={"vocab": (v + i) % group}, device_id_type=MESH)
    for i in range(1, data):
        pl.semaphore_signal(barrier, inc=1, device_id={"dp": (d + i) % data}, device_id_type=MESH)
    emb_copy = []
    for k in range(data):
        j = order[k]
        copy = pltpu.make_async_copy(embed_hbm.at[:, columns(j)], emb.at[j], emb_sem.at[k])
        copy.start()
        emb_copy.append(copy)
    own_copy.wait()
    pl.semaphore_wait(barrier, group - 1 + data - 1)

    pending = []
    gz, place = [], []
    for k in range(data):
        j = order[k]
        copy = pltpu.make_async_copy(own.at[:, columns(j)], gath.at[j, a, b], place_sem.at[k])
        copy.start()
        place.append(copy)
        hops = []
        for i in range(1, outer):
            copy = remote(
                own.at[:, columns(j)], gath.at[j, a, b], gz_s.at[k, i - 1], gz_r.at[k, i - 1],
                vocab=at_outer(i),
            )
            copy.start()
            hops.append(copy)
        gz.append(hops)
        pending += hops

    tgt_copy.wait()
    bits_copy.wait()
    row_id = lax.broadcasted_iota(jnp.int32, (tokens, tokens), 0)
    col_id = lax.broadcasted_iota(jnp.int32, (tokens, tokens), 1)
    eye = row_id == col_id

    def to_column(row):
        return jnp.sum(jnp.where(eye, jnp.broadcast_to(row, (tokens, tokens)), 0.0), axis=1, keepdims=True)

    def to_row(column):
        return jnp.sum(jnp.where(eye, jnp.broadcast_to(column, (tokens, tokens)), 0.0), axis=0, keepdims=True)

    target = to_column(tgt[...].astype(f32))
    lane = lax.broadcasted_iota(jnp.int32, (tokens, 128), 1)
    shift = lane & 31
    slot = lane // 32
    for tile in range(vocab_local // 128):
        word = jnp.broadcast_to(bits[:, 4 * tile:4 * tile + 1], (tokens, 128))
        for w in range(1, 4):
            piece = jnp.broadcast_to(bits[:, 4 * tile + w:4 * tile + w + 1], (tokens, 128))
            word = jnp.where(slot == w, piece, word)
        set_bit = lax.shift_right_arithmetic(word, shift) & 1
        ids = (lane + (v * vocab_local + tile * 128)).astype(f32)
        is_target = jnp.where(ids == target, 1.0, 0.0)
        span = slice(tile * 128, tile * 128 + 128)
        hot[:, span] = is_target
        allow[:, span] = jnp.maximum(set_bit.astype(f32), is_target)
    stat[...] = jnp.zeros(stat.shape, f32)

    gy = []
    for k in range(data):
        j = order[k]
        place[k].wait()
        for copy in gz[k]:
            copy.wait_recv()
        hops = []
        for i in range(1, inner):
            copy = remote(
                gath.at[j, :, b], gath.at[j, :, b], gy_s.at[k, i - 1], gy_r.at[k, i - 1],
                vocab=at_inner(i),
            )
            copy.start()
            hops.append(copy)
        gy.append(hops)
        pending += hops

    scores = jnp.zeros((tokens, vocab_local), f32)
    gd = []
    for k in range(data):
        j = order[k]
        for copy in gy[k]:
            copy.wait_recv()
        if k < data - 1:
            copy = remote(gath.at[j], cols.at[k], gd_s.at[k], gd_r.at[k], dp=j)
            copy.start()
            gd.append(copy)
            pending.append(copy)
        block = gath[j].astype(f32).reshape(tokens, width).astype(bf16)
        if k == data - 1:
            h2[data - 1] = block
        emb_copy[k].wait()
        scores += lax.dot_general(block, emb[j], (((1,), (1,)), ((), ())), preferred_element_type=f32)

    bent = jnp.tanh(scores / softcap)
    capped = softcap * bent
    hot_now = hot[...]
    weight = jnp.where(allow[...] > 0.0, jnp.exp(capped), 0.0)
    stat[0:1, 0:tokens] = to_row(jnp.sum(weight, axis=1, keepdims=True))
    stat[1:2, 0:tokens] = to_row(jnp.sum(hot_now * capped, axis=1, keepdims=True))
    st = []
    for i in range(1, group):
        copy = remote(stat, stat_in.at[i - 1], st_s.at[i - 1], st_r.at[i - 1], vocab=(v + i) % group)
        copy.start()
        st.append(copy)
    pending += st
    slope = 1.0 - jnp.square(bent)
    summed = stat[...]
    for i in range(1, group):
        st[i - 1].wait_recv()
        summed = summed + stat_in[i - 1]
    sums = summed[0:1, 0:tokens]
    loss_ref[...] = jnp.log(sums) - summed[1:2, 0:tokens]
    share = to_column(1.0 / sums)
    dlogit = ((weight * share - hot_now) * slope).astype(bf16)
    dl[data - 1] = dlogit

    dx, ry = [], []
    for k in range(data):
        part[k] = jnp.dot(dlogit, emb[k], preferred_element_type=f32).reshape(outer, inner, rows, width)
        hops = []
        for i in range(1, inner):
            mine = part[k, :, (b + i) % inner].reshape(outer * rows, width)
            y_out[k, i - 1] = mine.astype(bf16)
            copy = remote(
                y_out.at[k, i - 1], y_in.at[k, i - 1], ry_s.at[k, i - 1], ry_r.at[k, i - 1],
                vocab=at_inner(i),
            )
            copy.start()
            hops.append(copy)
        ry.append(hops)
        pending += hops
        if k == 0:
            for i in range(data - 1):
                copy = remote(
                    dl.at[data - 1], dl.at[i], dl_s.at[i], dl_r.at[i], dp=(d + 1 + i) % data
                )
                copy.start()
                dx.append(copy)
            pending += dx

    rz = []
    for k in range(data):
        now = part[k, :, b]
        for i in range(1, inner):
            ry[k][i - 1].wait_recv()
            now = now + y_in[k, i - 1].astype(f32).reshape(outer, rows, width)
        total[k] = now
        hops = []
        for i in range(1, outer):
            z_out[k, i - 1] = total[k, (a + i) % outer].astype(bf16)
            copy = remote(
                z_out.at[k, i - 1], z_in.at[k, i - 1], rz_s.at[k, i - 1], rz_r.at[k, i - 1],
                vocab=at_outer(i),
            )
            copy.start()
            hops.append(copy)
        rz.append(hops)
        pending += hops

    for k in range(data - 1):
        gd[k].wait_recv()
        h2[k] = cols[k].astype(f32).reshape(tokens, width).astype(bf16)
        dx[k].wait_recv()
    everything = h2[...].reshape(data * tokens, width)
    out_copies = []
    for tile in range(vocab_local // 128):
        span = slice(tile * 128, tile * 128 + 128)
        left = dl[:, :, span].reshape(data * tokens, 128)
        egrad[span, :] = lax.dot_general(
            left, everything, (((0,), (0,)), ((), ())), preferred_element_type=f32
        )
        copy = pltpu.make_async_copy(egrad.at[span], egrad_hbm.at[span], egrad_sem.at[tile])
        copy.start()
        out_copies.append(copy)

    for k in range(data):
        now = total[k, a]
        for i in range(1, outer):
            rz[k][i - 1].wait_recv()
            now = now + z_in[k, i - 1].astype(f32)
        hgrad_ref[:, k * width:(k + 1) * width] = now
    for copy in pending:
        copy.wait_send()
    for copy in out_copies:
        copy.wait()


def on_device(data, group, hidden, embedding, targets, grammar_bits):
    inner = 1 << ((group.bit_length() - 1) // 2)
    outer = group // inner
    rows, depth = hidden.shape
    vocab_local = embedding.shape[0]
    width = depth // data
    tokens = rows * group
    lanes = -(-tokens // 128) * 128
    more_in, more_out = max(inner - 1, 1), max(outer - 1, 1)
    dma = pltpu.SemaphoreType.DMA
    vmem = pltpu.VMEM
    anywhere = pl.BlockSpec(memory_space=pl.ANY)
    inside = pl.BlockSpec(memory_space=pltpu.VMEM)
    loss, hidden_grad, embed_grad = pl.pallas_call(
        functools.partial(kernel, data, outer, inner),
        out_shape=(
            jax.ShapeDtypeStruct((1, tokens), f32),
            jax.ShapeDtypeStruct((rows, depth), f32),
            jax.ShapeDtypeStruct((vocab_local, width), f32),
        ),
        in_specs=[anywhere] * 4,
        out_specs=(inside, inside, anywhere),
        scratch_shapes=[
            vmem((rows, depth), bf16),
            vmem((data, vocab_local, width), bf16),
            vmem((1, tokens), jnp.int32),
            vmem(grammar_bits.shape, jnp.int32),
            vmem((data, outer, inner, rows, width), bf16),
            vmem((data - 1, outer, inner, rows, width), bf16),
            vmem((data, tokens, vocab_local), bf16),
            vmem((data, tokens, width), bf16),
            vmem((2, lanes), f32),
            vmem((group - 1, 2, lanes), f32),
            vmem((data, outer, inner, rows, width), f32),
            vmem((data, more_in, outer * rows, width), bf16),
            vmem((data, more_in, outer * rows, width), bf16),
            vmem((data, outer, rows, width), f32),
            vmem((data, more_out, rows, width), bf16),
            vmem((data, more_out, rows, width), bf16),
            vmem((vocab_local, width), f32),
            vmem((tokens, vocab_local), f32),
            vmem((tokens, vocab_local), f32),
            dma((3,)), dma((data,)), dma((data,)), dma((vocab_local // 128,)),
            dma((data, more_out)), dma((data, more_out)),
            dma((data, more_in)), dma((data, more_in)),
            dma((data - 1,)), dma((data - 1,)),
            dma((group - 1,)), dma((group - 1,)),
            dma((data - 1,)), dma((data - 1,)),
            dma((data, more_in)), dma((data, more_in)),
            dma((data, more_out)), dma((data, more_out)),
        ],
        compiler_params=pltpu.CompilerParams(
            collective_id=0, has_side_effects=True, vmem_limit_bytes=60 * 2**20
        ),
    )(hidden, embedding, targets.reshape(1, tokens), grammar_bits)
    return loss.reshape(tokens), hidden_grad, embed_grad


def solution(mesh):
    in_specs = (P(("dp", "vocab"), None), P("vocab", None), P("dp"), P("dp", "vocab"))
    out_specs = (P("dp"), P(("dp", "vocab"), None), P("vocab", "dp"))
    body = functools.partial(on_device, mesh.shape["dp"], mesh.shape["vocab"])
    return jax.shard_map(body, mesh=mesh, in_specs=in_specs, out_specs=out_specs, check_vma=False)
```

time: 143 us -> 41.2 us (0.29)
  blocking collectives: 93.4 us -> 0 us
  Pallas kernels: 0 us -> 33 us
  waiting for transfers between devices: 20.3 us -> 0 us
  between operations: 14.1 us -> 0.64 us
  matrix products: 10.2 us -> 0 us
  local copies, waits for them, and re-layouts: 0.93 us -> 7.33 us
  starting transfers between devices: 3.34 us -> 0 us
    all_gather x3 -> x0, blocking collectives: 72 us -> none  [the longest x1 33.5 us: on_device(): gathered = lax.all_gather(hidden, 'vocab', axis=0, tiled=True)]
    pallas_call x0 -> x1, Pallas kernels: none -> 33 us  [on_device(): pl.pallas_call(functools.partial(kernel, data, outer, inner), out_shape=(...]
    psum x1 -> x0, blocking collectives: 21.5 us -> none  [on_device(): totals, target_logit = lax.psum((local_total, local_target), 'vocab')]
    reduce_scatter x1 -> x0, waiting for transfers between devices: 20.3 us -> none  [on_device(): lax.psum_scatter(jnp.dot(dlogit, embedding, preferred_element_type=jnp.fl...]
    dot_general x3 -> x0, matrix products: 10.2 us -> none  [the longest x1 4.28 us: on_device(): jnp.dot(dlogit, embedding, preferred_element_type=jnp.float32)]
    unnamed x2 -> x4, local copies, waits for them, and re-layouts: 0.01 us -> 7.33 us
    all_to_all x1 -> x0, starting transfers between devices: 3.3 us -> none  [on_device(): lax.all_to_all(hidden, 'dp', split_axis=1, concat_axis=0, tiled=True)]
  transfers between devices with their start and end apart: 2 -> 0, of which waited for: 1 -> 0; matrix products, arithmetic and copies ran while one was open for 1% -> 0% of each run, Pallas kernels for 0% -> 0%
where the time goes in v1:
time: 41.2 us; the launch traced here: 41 us
  Pallas kernels  33 us (80%)
  local copies, waits for them, and re-layouts  7.33 us (18%)
  between operations  0.64 us (2%)
    pallas_call x1, Pallas kernels, on_device(): pl.pallas_call(functools.partial(kernel, data, outer, inner), out_shape=(...  33 us
    unnamed x4, local copies, waits for them, and re-layouts  7.33 us

profile of v1, /device:TPU:0, one launch (start us, length us, event | category | flops | bytes accessed | tf_op | source)
XLA Modules:
  0.0 41.0 jit_solution(15549274388909182814)
XLA Ops:
  0.6 1.4 %copy.7.bits_hbm = s32[64,16]{1,0:T(8,128)} copy(s32[64,16]{0,1:T(8,128)} %param.7) | data formatting | bytes 8192 | tf_op args[3]
  2.0 33.0 %shard_map.67 = (f32[1,64]{1,0:T(1,128)}, f32[8,4608]{1,0:T(8,128)}, f32[512,1152]{1,0:T(8,128)}) custom-call(bf16[8,4608]{1,0:T(8,128)(2,1)} %hidden_hbm.1, bf16[512,4608]{1,0:T(8,128)(2,1)} %embed_hbm.1, s32[1,64]{1,0:T(1,128)} %bitcast.2, s32[64,16]{1,0:T(8,128)} %copy.7.bits_hbm), custom_call_target="tpu_custom_call" | custom-call | tf_op jit(solution)/shard_map/pallas_call | solution.py:258
  35.0 1.1 %copy.11 = f32[64]{0:T(128)} copy(f32[64]{0:T(128)} %bitcast.3) | data formatting | bytes 512
  36.2 1.6 %copy.12 = f32[8,4608]{1,0:T(8,128)} copy(f32[8,4608]{1,0:T(8,128)} %get-tuple-element.13) | data formatting | bytes 294912
  37.7 3.2 %copy.13 = f32[512,1152]{1,0:T(8,128)} copy(f32[512,1152]{1,0:T(8,128)} %get-tuple-element.14) | data formatting | bytes 4718592

commit v2 on v1

--- a/solution.py
+++ b/solution.py
@@ -16,10 +16,10 @@
 def kernel(
     data, outer, inner,
     hidden_hbm, embed_hbm, targets_hbm, bits_hbm,
-    loss_ref, hgrad_ref, egrad_hbm,
+    loss_ref, hgrad_ref, egrad,
     own, emb, tgt, bits, gath, cols, dl, h2, stat, stat_in,
-    part, y_out, y_in, total, z_out, z_in, egrad, allow, hot,
-    local_sem, emb_sem, place_sem, egrad_sem,
+    part, y_out, y_in, total, z_out, z_in, allow, hot,
+    local_sem, emb_sem, place_sem,
     gz_s, gz_r, gy_s, gy_r, gd_s, gd_r, st_s, st_r, dl_s, dl_r,
     ry_s, ry_r, rz_s, rz_r,
 ):
@@ -101,10 +101,11 @@
     lane = lax.broadcasted_iota(jnp.int32, (tokens, 128), 1)
     shift = lane & 31
     slot = lane // 32
+    words = bits[...].T
     for tile in range(vocab_local // 128):
-        word = jnp.broadcast_to(bits[:, 4 * tile:4 * tile + 1], (tokens, 128))
+        word = jnp.broadcast_to(words[:, 4 * tile:4 * tile + 1], (tokens, 128))
         for w in range(1, 4):
-            piece = jnp.broadcast_to(bits[:, 4 * tile + w:4 * tile + w + 1], (tokens, 128))
+            piece = jnp.broadcast_to(words[:, 4 * tile + w:4 * tile + w + 1], (tokens, 128))
             word = jnp.where(slot == w, piece, word)
         set_bit = lax.shift_right_arithmetic(word, shift) & 1
         ids = (lane + (v * vocab_local + tile * 128)).astype(f32)
@@ -219,16 +220,12 @@
         h2[k] = cols[k].astype(f32).reshape(tokens, width).astype(bf16)
         dx[k].wait_recv()
     everything = h2[...].reshape(data * tokens, width)
-    out_copies = []
     for tile in range(vocab_local // 128):
         span = slice(tile * 128, tile * 128 + 128)
         left = dl[:, :, span].reshape(data * tokens, 128)
         egrad[span, :] = lax.dot_general(
             left, everything, (((0,), (0,)), ((), ())), preferred_element_type=f32
         )
-        copy = pltpu.make_async_copy(egrad.at[span], egrad_hbm.at[span], egrad_sem.at[tile])
-        copy.start()
-        out_copies.append(copy)
 
     for k in range(data):
         now = total[k, a]
@@ -238,7 +235,14 @@
         hgrad_ref[:, k * width:(k + 1) * width] = now
     for copy in pending:
         copy.wait_send()
-    for copy in out_copies:
+
+
+def write_out(loss, hgrad, egrad, loss_out, hgrad_out, egrad_out, sems):
+    pairs = [(egrad, egrad_out), (hgrad, hgrad_out), (loss, loss_out)]
+    copies = [pltpu.make_async_copy(src, dst, sems.at[i]) for i, (src, dst) in enumerate(pairs)]
+    for copy in copies:
+        copy.start()
+    for copy in copies:
         copy.wait()
 
 
@@ -253,22 +257,23 @@
     more_in, more_out = max(inner - 1, 1), max(outer - 1, 1)
     dma = pltpu.SemaphoreType.DMA
     vmem = pltpu.VMEM
-    anywhere = pl.BlockSpec(memory_space=pl.ANY)
+    anywhere = pl.BlockSpec(memory_space=pltpu.HBM)
     inside = pl.BlockSpec(memory_space=pltpu.VMEM)
+    operands = (hidden, embedding, targets.reshape(1, tokens), grammar_bits.T)
     loss, hidden_grad, embed_grad = pl.pallas_call(
         functools.partial(kernel, data, outer, inner),
         out_shape=(
-            jax.ShapeDtypeStruct((1, tokens), f32),
-            jax.ShapeDtypeStruct((rows, depth), f32),
-            jax.ShapeDtypeStruct((vocab_local, width), f32),
+            vmem((1, tokens), f32),
+            vmem((rows, depth), f32),
+            vmem((vocab_local, width), f32),
         ),
         in_specs=[anywhere] * 4,
-        out_specs=(inside, inside, anywhere),
+        out_specs=(inside, inside, inside),
         scratch_shapes=[
             vmem((rows, depth), bf16),
             vmem((data, vocab_local, width), bf16),
             vmem((1, tokens), jnp.int32),
-            vmem(grammar_bits.shape, jnp.int32),
+            vmem(grammar_bits.shape[::-1], jnp.int32),
             vmem((data, outer, inner, rows, width), bf16),
             vmem((data - 1, outer, inner, rows, width), bf16),
             vmem((data, tokens, vocab_local), bf16),
@@ -281,10 +286,9 @@
             vmem((data, outer, rows, width), f32),
             vmem((data, more_out, rows, width), bf16),
             vmem((data, more_out, rows, width), bf16),
-            vmem((vocab_local, width), f32),
             vmem((tokens, vocab_local), f32),
             vmem((tokens, vocab_local), f32),
-            dma((3,)), dma((data,)), dma((data,)), dma((vocab_local // 128,)),
+            dma((3,)), dma((data,)), dma((data,)),
             dma((data, more_out)), dma((data, more_out)),
             dma((data, more_in)), dma((data, more_in)),
             dma((data - 1,)), dma((data - 1,)),
@@ -294,9 +298,16 @@
             dma((data, more_out)), dma((data, more_out)),
         ],
         compiler_params=pltpu.CompilerParams(
-            collective_id=0, has_side_effects=True, vmem_limit_bytes=60 * 2**20
+            collective_id=0, has_side_effects=True, vmem_limit_bytes=48 * 2**20
         ),
-    )(hidden, embedding, targets.reshape(1, tokens), grammar_bits)
+    )(*(pltpu.with_memory_space_constraint(x, pltpu.HBM) for x in operands))
+    loss, hidden_grad, embed_grad = pl.pallas_call(
+        write_out,
+        out_shape=tuple(jax.ShapeDtypeStruct(x.shape, f32) for x in (loss, hidden_grad, embed_grad)),
+        in_specs=[inside] * 3,
+        out_specs=(anywhere,) * 3,
+        scratch_shapes=[dma((3,))],
+    )(*(pltpu.with_memory_space_constraint(x, pltpu.VMEM) for x in (loss, hidden_grad, embed_grad)))
     return loss.reshape(tokens), hidden_grad, embed_grad
 
 

time: 41.2 us -> 34.7 us (0.84)
  local copies, waits for them, and re-layouts: 7.33 us -> 0 us
  Pallas kernels: 33 us -> 33.9 us
    unnamed x4 -> x0, local copies, waits for them, and re-layouts: 7.33 us -> none
    pallas_call x0 -> x1, Pallas kernels: none -> 1.47 us  [on_device(): pl.pallas_call(write_out, out_shape=tuple((jax.ShapeDtypeStruct(x.shape,...]
    pallas_call x1, Pallas kernels: 33 us -> 32.4 us  [on_device(): pl.pallas_call(functools.partial(kernel, data, outer, inner), out_shape=(...]
where the time goes in v2:
time: 34.7 us; the launch traced here: 34.6 us
  Pallas kernels  33.9 us (98%)
  between operations  0.64 us (2%)
    pallas_call x1, Pallas kernels, on_device(): pl.pallas_call(functools.partial(kernel, data, outer, inner), out_shape=(...  32.4 us
    pallas_call x1, Pallas kernels, on_device(): pl.pallas_call(write_out, out_shape=tuple((jax.ShapeDtypeStruct(x.shape,...  1.47 us

profile of v2, /device:TPU:0, one launch (start us, length us, event | category | flops | bytes accessed | tf_op | source)
XLA Modules:
  0.0 34.6 jit_solution(14968256052348872271)
XLA Ops:
  0.6 32.4 %shard_map.67 = (f32[1,64]{1,0:T(1,128)S(1)}, f32[8,4608]{1,0:T(8,128)S(1)}, f32[512,1152]{1,0:T(8,128)S(1)}) custom-call(bf16[8,4608]{1,0:T(8,128)(2,1)} %hidden_hbm.1, bf16[512,4608]{1,0:T(8,128)(2,1)} %embed_hbm.1, s32[1,64]{1,0:T(1,128)} %bitcast.4, s32[16,64]{1,0:T(8,128)} %bitcast.3), custom_call_target="tpu_custom_call" | custom-call | tf_op jit(solution)/shard_map/pallas_call | solution.py:263
  33.1 1.5 %shard_map.68 = (f32[1,64]{1,0:T(1,128)}, f32[8,4608]{1,0:T(8,128)}, f32[512,1152]{1,0:T(8,128)}) custom-call(f32[1,64]{1,0:T(1,128)S(1)} %get-tuple-element.9.loss, f32[8,4608]{1,0:T(8,128)S(1)} %get-tuple-element.10.hgrad, f32[512,1152]{1,0:T(8,128)S(1)} %get-tuple-element.11.egrad), custom_call_target="tpu_custom_call" | custom-call | tf_op jit(solution)/shard_map/pallas_call | solution.py:304

commit v3 on v2

--- a/solution.py
+++ b/solution.py
@@ -20,7 +20,7 @@
     own, emb, tgt, bits, gath, cols, dl, h2, stat, stat_in,
     part, y_out, y_in, total, z_out, z_in, allow, hot,
     local_sem, emb_sem, place_sem,
-    gz_s, gz_r, gy_s, gy_r, gd_s, gd_r, st_s, st_r, dl_s, dl_r,
+    gz_s, gz_r, go_s, go_r, gy_s, gy_r, gd_s, gd_r, st_s, st_r, dl_s, dl_r,
     ry_s, ry_r, rz_s, rz_r,
 ):
     d = lax.axis_index("dp")
@@ -67,22 +67,38 @@
     own_copy.wait()
     pl.semaphore_wait(barrier, group - 1 + data - 1)
 
+    half = (width // 128 + 1) // 2 * 128
+    halves = [(0, half), (half, width - half)]
+    pieces = [(k, h) for k in range(data) for h in range(2)]
     pending = []
-    gz, place = [], []
+    gz, go, place = [], [], []
     for k in range(data):
         j = order[k]
-        copy = pltpu.make_async_copy(own.at[:, columns(j)], gath.at[j, a, b], place_sem.at[k])
+        copy = pltpu.make_async_copy(own.at[:, columns(j)], gath.at[j, 0, b], place_sem.at[k])
         copy.start()
         place.append(copy)
+        for h in range(2):
+            start, size = halves[h]
+            source = own.at[:, pl.ds(pl.multiple_of(j * width + start, 128), size)]
+            hops = []
+            for i in range(1, outer):
+                copy = remote(
+                    source, gath.at[j, i, b, :, pl.ds(start, size)],
+                    gz_s.at[2 * k + h, i - 1], gz_r.at[2 * k + h, i - 1], vocab=at_outer(i),
+                )
+                copy.start()
+                hops.append(copy)
+            gz.append(hops)
+            pending += hops
         hops = []
-        for i in range(1, outer):
+        for i in range(1, inner):
             copy = remote(
-                own.at[:, columns(j)], gath.at[j, a, b], gz_s.at[k, i - 1], gz_r.at[k, i - 1],
-                vocab=at_outer(i),
+                own.at[:, columns(j)], gath.at[j, 0, b], go_s.at[k, i - 1], go_r.at[k, i - 1],
+                vocab=at_inner(i),
             )
             copy.start()
             hops.append(copy)
-        gz.append(hops)
+        go.append(hops)
         pending += hops
 
     tgt_copy.wait()
@@ -115,39 +131,53 @@
         allow[:, span] = jnp.maximum(set_bit.astype(f32), is_target)
     stat[...] = jnp.zeros(stat.shape, f32)
 
-    gy = []
-    for k in range(data):
-        j = order[k]
-        place[k].wait()
-        for copy in gz[k]:
-            copy.wait_recv()
-        hops = []
-        for i in range(1, inner):
-            copy = remote(
-                gath.at[j, :, b], gath.at[j, :, b], gy_s.at[k, i - 1], gy_r.at[k, i - 1],
-                vocab=at_inner(i),
+    def in_order(block, span):
+        found = [
+            block[(a - i + outer) % outer, :, :, span].astype(f32).reshape(inner * rows, -1)
+            for i in range(outer)
+        ]
+        return jnp.concatenate(found, axis=0).astype(bf16)
+
+    gy, gd = [], []
+    scores = jnp.zeros((tokens, vocab_local), f32)
+    behind = 3
+    for q in range(len(pieces) + behind):
+        if q < len(pieces):
+            k, h = pieces[q]
+            span = pl.ds(*halves[h])
+            for copy in gz[q]:
+                copy.wait_recv()
+            hops = []
+            for i in range(1, inner):
+                passed = gath.at[order[k], pl.ds(1, outer - 1), b, :, span]
+                copy = remote(passed, passed, gy_s.at[q, i - 1], gy_r.at[q, i - 1], vocab=at_inner(i))
+                copy.start()
+                hops.append(copy)
+            gy.append(hops)
+            pending += hops
+        if q >= behind:
+            k, h = pieces[q - behind]
+            j = order[k]
+            start, size = halves[h]
+            span = slice(start, start + size)
+            if h == 0:
+                place[k].wait()
+                for copy in go[k]:
+                    copy.wait_recv()
+                emb_copy[k].wait()
+            for copy in gy[q - behind]:
+                copy.wait_recv()
+            if h == 1 and k < data - 1:
+                copy = remote(gath.at[j], cols.at[k], gd_s.at[k], gd_r.at[k], dp=j)
+                copy.start()
+                gd.append(copy)
+                pending.append(copy)
+            block = in_order(gath.at[j], span)
+            if k == data - 1:
+                h2[data - 1, :, span] = block
+            scores += lax.dot_general(
+                block, emb[j, :, span], (((1,), (1,)), ((), ())), preferred_element_type=f32
             )
-            copy.start()
-            hops.append(copy)
-        gy.append(hops)
-        pending += hops
-
-    scores = jnp.zeros((tokens, vocab_local), f32)
-    gd = []
-    for k in range(data):
-        j = order[k]
-        for copy in gy[k]:
-            copy.wait_recv()
-        if k < data - 1:
-            copy = remote(gath.at[j], cols.at[k], gd_s.at[k], gd_r.at[k], dp=j)
-            copy.start()
-            gd.append(copy)
-            pending.append(copy)
-        block = gath[j].astype(f32).reshape(tokens, width).astype(bf16)
-        if k == data - 1:
-            h2[data - 1] = block
-        emb_copy[k].wait()
-        scores += lax.dot_general(block, emb[j], (((1,), (1,)), ((), ())), preferred_element_type=f32)
 
     bent = jnp.tanh(scores / softcap)
     capped = softcap * bent
@@ -173,21 +203,25 @@
     dl[data - 1] = dlogit
 
     dx, ry = [], []
-    for k in range(data):
-        part[k] = jnp.dot(dlogit, emb[k], preferred_element_type=f32).reshape(outer, inner, rows, width)
+    for q, (k, h) in enumerate(pieces):
+        start, size = halves[h]
+        span = slice(start, start + size)
+        part[k, :, :, :, span] = jnp.dot(
+            dlogit, emb[k, :, span], preferred_element_type=f32
+        ).reshape(outer, inner, rows, size)
         hops = []
         for i in range(1, inner):
-            mine = part[k, :, (b + i) % inner].reshape(outer * rows, width)
-            y_out[k, i - 1] = mine.astype(bf16)
+            mine = part[k, :, (b + i) % inner, :, span].reshape(outer * rows, size)
+            y_out[k, i - 1, :, span] = mine.astype(bf16)
             copy = remote(
-                y_out.at[k, i - 1], y_in.at[k, i - 1], ry_s.at[k, i - 1], ry_r.at[k, i - 1],
-                vocab=at_inner(i),
+                y_out.at[k, i - 1, :, pl.ds(start, size)], y_in.at[k, i - 1, :, pl.ds(start, size)],
+                ry_s.at[q, i - 1], ry_r.at[q, i - 1], vocab=at_inner(i),
             )
             copy.start()
             hops.append(copy)
         ry.append(hops)
         pending += hops
-        if k == 0:
+        if q == 0:
             for i in range(data - 1):
                 copy = remote(
                     dl.at[data - 1], dl.at[i], dl_s.at[i], dl_r.at[i], dp=(d + 1 + i) % data
@@ -197,18 +231,20 @@
             pending += dx
 
     rz = []
-    for k in range(data):
-        now = part[k, :, b]
+    for q, (k, h) in enumerate(pieces):
+        start, size = halves[h]
+        span = slice(start, start + size)
+        now = part[k, :, b, :, span]
         for i in range(1, inner):
-            ry[k][i - 1].wait_recv()
-            now = now + y_in[k, i - 1].astype(f32).reshape(outer, rows, width)
-        total[k] = now
+            ry[q][i - 1].wait_recv()
+            now = now + y_in[k, i - 1, :, span].astype(f32).reshape(outer, rows, size)
+        total[k, :, :, span] = now
         hops = []
         for i in range(1, outer):
-            z_out[k, i - 1] = total[k, (a + i) % outer].astype(bf16)
+            z_out[k, i - 1, :, span] = total[k, (a + i) % outer, :, span].astype(bf16)
             copy = remote(
-                z_out.at[k, i - 1], z_in.at[k, i - 1], rz_s.at[k, i - 1], rz_r.at[k, i - 1],
-                vocab=at_outer(i),
+                z_out.at[k, i - 1, :, pl.ds(start, size)], z_in.at[k, i - 1, :, pl.ds(start, size)],
+                rz_s.at[q, i - 1], rz_r.at[q, i - 1], vocab=at_outer(i),
             )
             copy.start()
             hops.append(copy)
@@ -217,7 +253,7 @@
 
     for k in range(data - 1):
         gd[k].wait_recv()
-        h2[k] = cols[k].astype(f32).reshape(tokens, width).astype(bf16)
+        h2[k] = in_order(cols.at[k], slice(0, width))
         dx[k].wait_recv()
     everything = h2[...].reshape(data * tokens, width)
     for tile in range(vocab_local // 128):
@@ -227,12 +263,14 @@
             left, everything, (((0,), (0,)), ((), ())), preferred_element_type=f32
         )
 
-    for k in range(data):
-        now = total[k, a]
+    for q, (k, h) in enumerate(pieces):
+        start, size = halves[h]
+        span = slice(start, start + size)
+        now = total[k, a, :, span]
         for i in range(1, outer):
-            rz[k][i - 1].wait_recv()
-            now = now + z_in[k, i - 1].astype(f32)
-        hgrad_ref[:, k * width:(k + 1) * width] = now
+            rz[q][i - 1].wait_recv()
+            now = now + z_in[k, i - 1, :, span].astype(f32)
+        hgrad_ref[:, k * width + start:k * width + start + size] = now
     for copy in pending:
         copy.wait_send()
 
@@ -289,13 +327,14 @@
             vmem((tokens, vocab_local), f32),
             vmem((tokens, vocab_local), f32),
             dma((3,)), dma((data,)), dma((data,)),
-            dma((data, more_out)), dma((data, more_out)),
+            dma((2 * data, more_out)), dma((2 * data, more_out)),
             dma((data, more_in)), dma((data, more_in)),
+            dma((2 * data, more_in)), dma((2 * data, more_in)),
             dma((data - 1,)), dma((data - 1,)),
             dma((group - 1,)), dma((group - 1,)),
             dma((data - 1,)), dma((data - 1,)),
-            dma((data, more_in)), dma((data, more_in)),
-            dma((data, more_out)), dma((data, more_out)),
+            dma((2 * data, more_in)), dma((2 * data, more_in)),
+            dma((2 * data, more_out)), dma((2 * data, more_out)),
         ],
         compiler_params=pltpu.CompilerParams(
             collective_id=0, has_side_effects=True, vmem_limit_bytes=48 * 2**20

time: 34.7 us -> 36.1 us (1.040)
  Pallas kernels: 33.9 us -> 35.3 us
    pallas_call x1, Pallas kernels: 32.4 us -> 33.9 us  [on_device(): pl.pallas_call(functools.partial(kernel, data, outer, inner), out_shape=(...]
where the time goes in v3:
time: 36.1 us; the launch traced here: 36 us
  Pallas kernels  35.3 us (98%)
  between operations  0.64 us (2%)
    pallas_call x1, Pallas kernels, on_device(): pl.pallas_call(functools.partial(kernel, data, outer, inner), out_shape=(...  33.9 us
    pallas_call x1, Pallas kernels, on_device(): pl.pallas_call(write_out, out_shape=tuple((jax.ShapeDtypeStruct(x.shape,...  1.47 us

profile of v3, /device:TPU:0, one launch (start us, length us, event | category | flops | bytes accessed | tf_op | source)
XLA Modules:
  0.0 36.0 jit_solution(9036602144757187940)
XLA Ops:
  0.6 33.9 %shard_map.67 = (f32[1,64]{1,0:T(1,128)S(1)}, f32[8,4608]{1,0:T(8,128)S(1)}, f32[512,1152]{1,0:T(8,128)S(1)}) custom-call(bf16[8,4608]{1,0:T(8,128)(2,1)} %hidden_hbm.1, bf16[512,4608]{1,0:T(8,128)(2,1)} %embed_hbm.1, s32[1,64]{1,0:T(1,128)} %bitcast.4, s32[16,64]{1,0:T(8,128)} %bitcast.3), custom_call_target="tpu_custom_call" | custom-call | tf_op jit(solution)/shard_map/pallas_call | solution.py:301
  34.5 1.5 %shard_map.68 = (f32[1,64]{1,0:T(1,128)}, f32[8,4608]{1,0:T(8,128)}, f32[512,1152]{1,0:T(8,128)}) custom-call(f32[1,64]{1,0:T(1,128)S(1)} %get-tuple-element.9.loss, f32[8,4608]{1,0:T(8,128)S(1)} %get-tuple-element.10.hgrad, f32[512,1152]{1,0:T(8,128)S(1)} %get-tuple-element.11.egrad), custom_call_target="tpu_custom_call" | custom-call | tf_op jit(solution)/shard_map/pallas_call | solution.py:343

commit v4 on v2

--- a/solution.py
+++ b/solution.py
@@ -115,39 +115,41 @@
         allow[:, span] = jnp.maximum(set_bit.astype(f32), is_target)
     stat[...] = jnp.zeros(stat.shape, f32)
 
-    gy = []
-    for k in range(data):
-        j = order[k]
-        place[k].wait()
-        for copy in gz[k]:
-            copy.wait_recv()
-        hops = []
-        for i in range(1, inner):
-            copy = remote(
-                gath.at[j, :, b], gath.at[j, :, b], gy_s.at[k, i - 1], gy_r.at[k, i - 1],
-                vocab=at_inner(i),
+    gy, gd = [], []
+    scores = jnp.zeros((tokens, vocab_local), f32)
+    behind = 2
+    for step in range(data + behind):
+        if step < data:
+            k, j = step, order[step]
+            place[k].wait()
+            for copy in gz[k]:
+                copy.wait_recv()
+            hops = []
+            for i in range(1, inner):
+                copy = remote(
+                    gath.at[j, :, b], gath.at[j, :, b], gy_s.at[k, i - 1], gy_r.at[k, i - 1],
+                    vocab=at_inner(i),
+                )
+                copy.start()
+                hops.append(copy)
+            gy.append(hops)
+            pending += hops
+        if step >= behind:
+            k, j = step - behind, order[step - behind]
+            for copy in gy[k]:
+                copy.wait_recv()
+            if k < data - 1:
+                copy = remote(gath.at[j], cols.at[k], gd_s.at[k], gd_r.at[k], dp=j)
+                copy.start()
+                gd.append(copy)
+                pending.append(copy)
+            block = gath[j].astype(f32).reshape(tokens, width).astype(bf16)
+            if k == data - 1:
+                h2[data - 1] = block
+            emb_copy[k].wait()
+            scores += lax.dot_general(
+                block, emb[j], (((1,), (1,)), ((), ())), preferred_element_type=f32
             )
-            copy.start()
-            hops.append(copy)
-        gy.append(hops)
-        pending += hops
-
-    scores = jnp.zeros((tokens, vocab_local), f32)
-    gd = []
-    for k in range(data):
-        j = order[k]
-        for copy in gy[k]:
-            copy.wait_recv()
-        if k < data - 1:
-            copy = remote(gath.at[j], cols.at[k], gd_s.at[k], gd_r.at[k], dp=j)
-            copy.start()
-            gd.append(copy)
-            pending.append(copy)
-        block = gath[j].astype(f32).reshape(tokens, width).astype(bf16)
-        if k == data - 1:
-            h2[data - 1] = block
-        emb_copy[k].wait()
-        scores += lax.dot_general(block, emb[j], (((1,), (1,)), ((), ())), preferred_element_type=f32)
 
     bent = jnp.tanh(scores / softcap)
     capped = softcap * bent
@@ -220,8 +222,10 @@
         h2[k] = cols[k].astype(f32).reshape(tokens, width).astype(bf16)
         dx[k].wait_recv()
     everything = h2[...].reshape(data * tokens, width)
-    for tile in range(vocab_local // 128):
-        span = slice(tile * 128, tile * 128 + 128)
+
+    @pl.loop(0, vocab_local // 128)
+    def _(tile):
+        span = pl.ds(pl.multiple_of(tile * 128, 128), 128)
         left = dl[:, :, span].reshape(data * tokens, 128)
         egrad[span, :] = lax.dot_general(
             left, everything, (((0,), (0,)), ((), ())), preferred_element_type=f32

time: 34.7 us -> 34.9 us (level)
  no operation moved by 1% of the time
where the time goes in v4:
time: 34.9 us; the launch traced here: 34.8 us
  Pallas kernels  34.2 us (98%)
  between operations  0.64 us (2%)
    pallas_call x1, Pallas kernels, on_device(): pl.pallas_call(functools.partial(kernel, data, outer, inner), out_shape=(...  32.7 us
    pallas_call x1, Pallas kernels, on_device(): pl.pallas_call(write_out, out_shape=tuple((jax.ShapeDtypeStruct(x.shape,...  1.47 us

profile of v4, /device:TPU:0, one launch (start us, length us, event | category | flops | bytes accessed | tf_op | source)
XLA Modules:
  0.0 34.8 jit_solution(7988408668410975023)
XLA Ops:
  0.6 32.7 %shard_map.67 = (f32[1,64]{1,0:T(1,128)S(1)}, f32[8,4608]{1,0:T(8,128)S(1)}, f32[512,1152]{1,0:T(8,128)S(1)}) custom-call(bf16[8,4608]{1,0:T(8,128)(2,1)} %hidden_hbm.1, bf16[512,4608]{1,0:T(8,128)(2,1)} %embed_hbm.1, s32[1,64]{1,0:T(1,128)} %bitcast.4, s32[16,64]{1,0:T(8,128)} %bitcast.3), custom_call_target="tpu_custom_call" | custom-call | tf_op jit(solution)/shard_map/pallas_call | solution.py:267
  33.3 1.5 %shard_map.68 = (f32[1,64]{1,0:T(1,128)}, f32[8,4608]{1,0:T(8,128)}, f32[512,1152]{1,0:T(8,128)}) custom-call(f32[1,64]{1,0:T(1,128)S(1)} %get-tuple-element.9.loss, f32[8,4608]{1,0:T(8,128)S(1)} %get-tuple-element.10.hgrad, f32[512,1152]{1,0:T(8,128)S(1)} %get-tuple-element.11.egrad), custom_call_target="tpu_custom_call" | custom-call | tf_op jit(solution)/shard_map/pallas_call | solution.py:308
